TPU v7x, 16 devices: a whole 2x2x2 slice. The times are simulated.
16 devices in a mesh: dp: 1, tp: 16 (over x, y, z, core).
Axes of the slice: x: 2, y: 2, z: 2, core: 2. Of those that a mesh axis runs over, the one named last changes fastest.
Arguments:
- x: bfloat16 [2048, 7168], P('dp')
- w_gate: bfloat16 [7168, 20480], P(None, 'tp')
- w_up: bfloat16 [7168, 20480], P(None, 'tp')
- w_down: bfloat16 [20480, 7168], P('tp')
Outputs:
- output: bfloat16 [2048, 7168], P('dp')
All inputs are finite; a program needn't handle non-finite values.
Results may differ from a plain program's by a relative error of at most 0.016.
Values are sent between devices in bfloat16 or wider.
A program may use at most 2 GiB of HBM per device.

v0:
```python
import jax
import jax.numpy as jnp
from jax import lax
from jax.sharding import PartitionSpec as P


def solution(mesh):
    def step(x, w_gate, w_up, w_down):
        gate = jnp.dot(x, w_gate, preferred_element_type=jnp.float32)
        up = jnp.dot(x, w_up, preferred_element_type=jnp.float32)
        hidden = (jax.nn.silu(gate) * up).astype(jnp.bfloat16)
        term = jnp.dot(hidden, w_down, preferred_element_type=jnp.float32).astype(jnp.bfloat16)
        return lax.psum(term, "tp")

    return jax.shard_map(
        step,
        mesh=mesh,
        in_specs=(P("dp", None), P(None, "tp"), P(None, "tp"), P("tp", None)),
        out_specs=P("dp", None),
        check_vma=False,
    )
```

profile of v0, /device:TPU:0, one launch (start us, length us, event | category | flops | bytes accessed | tf_op | source)
XLA Modules:
  0.0 459.7 jit_solution(7200914251567103437)
XLA Ops:
  6.5 0.0 all-reduce.2.cloned.1.call-start
  6.5 46.7 %fusion.1 = f32[2048,1280]{1,0:T(8,128)} fusion(bf16[2048,7168]{1,0:T(8,128)(2,1)} %param.4, bf16[7168,1280]{1,0:T(8,128)(2,1)} %param.5), kind=kOutput, calls=%fused_computation.3 | convolution fusion | flops 37580963840 | bytes 58195968 | tf_op jit(solution)/shard_map/dot_general | solution.py:9
  53.3 48.1 %fusion = bf16[2048,1280]{1,0:T(8,128)(2,1)S(1)} fusion(bf16[2048,7168]{1,0:T(8,128)(2,1)} %param.4, bf16[7168,1280]{1,0:T(8,128)(2,1)} %param.6, f32[2048,1280]{1,0:T(8,128)} %fusion.1), kind=kOutput, calls=%fused_computation.2 | convolution fusion | flops 37596692480 | bytes 63438848 | tf_op jit(solution)/shard_map/dot_general | solution.py:10
  101.3 46.9 %convolution_convert_fusion = bf16[2048,7168]{1,0:T(8,128)(2,1)} fusion(bf16[2048,1280]{1,0:T(8,128)(2,1)S(1)} %fusion, bf16[1280,7168]{1,0:T(8,128)(2,1)} %param.7), kind=kOutput, calls=%fused_computation | convolution fusion | flops 37595643904 | bytes 52953088 | tf_op jit(solution)/shard_map/dot_general | solution.py:12
  148.2 0.0 all-reduce.2.cloned.1.call-update
  148.3 284.5 %all-reduce.2.cloned.1.call-done = bf16[2048,7168]{1,0:T(8,128)(2,1)} async-done(((bf16[2048,7168]{1,0:T(8,128)(2,1)}), bf16[2048,7168]{1,0:T(8,128)(2,1)}) %all-reduce.2.cloned.1.call-update) | async-done | bytes 29360144 | tf_op jit(solution)/shard_map/psum | solution.py:13
  432.7 20.1 %copy.6 = bf16[2048,7168]{1,0:T(8,128)(2,1)} copy(bf16[2048,7168]{1,0:T(8,128)(2,1)} %all-reduce.2.cloned.1.call-done) | data formatting | bytes 58720256
Async XLA Ops:
  6.5 426.2 %all-reduce.2.cloned.1.call-start = ((), (), s32[]{:S(2)}) async-start(), calls=%async_computation | async-start | bytes 58720256 | tf_op jit(solution)/shard_map/psum | solution.py:13
Sparse Core Ops, SparseCore 0:
  148.4 284.3 all-reduce.1
where the time goes:
time: 460 us
  waiting for transfers between devices  284 us (62%)
  matrix products  142 us (31%)
  local copies, waits for them, and re-layouts  20.1 us (4%)
  between operations  13.4 us (3%)
    psum x1, waiting for transfers between devices, step(): return lax.psum(term, 'tp')  284 us
    dot_general x1, matrix products, step(): up = jnp.dot(x, w_up, preferred_element_type=jnp.float32)  48.1 us
    dot_general x1, matrix products, step(): jnp.dot(hidden, w_down, preferred_element_type=jnp.float32)  46.9 us
    dot_general x1, matrix products, step(): gate = jnp.dot(x, w_gate, preferred_element_type=jnp.float32)  46.7 us
    unnamed x1, local copies, waits for them, and re-layouts  20.1 us
  transfers between devices with their start and end apart: 1, of which 1 were waited for; matrix products, arithmetic and copies ran while one was open for 0% of the time, Pallas kernels for 0%

commit v1 on v0

v1 whole, which is shorter than its diff:
```python
import functools

import jax
import jax.numpy as jnp
from jax import lax
from jax.experimental import pallas as pl
from jax.experimental.pallas import tpu as pltpu
from jax.sharding import PartitionSpec as P

D = 7168
FF = 1280
M = 256
HALF = D // 2
OFF = (0, 1280, 2432)
WID = (1280, 1152, 1152)
GB = 256
NG = FF // GB
PC = M // 8
YS = 3
MESH = pl.DeviceIdType.MESH
F32 = jnp.float32
BF16 = jnp.bfloat16


def kernel(n, x_hbm, wg_hbm, wu_hbm, wd_hbm, y_hbm,
           xb, wgb, wub, wdb, hid, sb0, rb0, own, s1, r1, s2, r2, s3, r3, yo, yb,
           xsem, gsem, usem, dsem, osem,
           ss0, rs0, ss1, rs1, ss2, rs2, ss3, rs3, ssg, rsg, ssd, rsd):
    me = lax.axis_index("tp")
    core = me % 2
    sib = me + 1 - 2 * core
    bits = [(me // s) % 2 for s in (2, 4, 8)]
    prts = [me + s - 2 * s * ((me // s) % 2) for s in (2, 4, 8)]

    def pick(vals, axis):
        return (vals[0] * ((1 - axis) * (2 - axis) // 2) + vals[1] * (axis * (2 - axis))
                + vals[2] * (axis * (axis - 1) // 2))

    def geo(j, k):
        out = []
        for t in range(3):
            axis = (j + core + k + t) % 3
            out.append((pick(bits, axis), pick(prts, axis)))
        return out

    def rc(src, dst, ssem, rsem, dev):
        return pltpu.make_async_remote_copy(
            src_ref=src, dst_ref=dst, send_sem=ssem, recv_sem=rsem,
            device_id={"tp": dev}, device_id_type=MESH)

    def cols(k):
        return pl.ds(OFF[k], WID[k])

    def mo(v, m):
        return pl.multiple_of(v, m)

    def x_copy(i):
        return pltpu.make_async_copy(
            x_hbm.at[pl.ds(mo(i * M, M), M), :], xb.at[i % 2], xsem.at[i % 2])

    def g_copies(u):
        c = pl.ds(mo((u % NG) * GB, GB), GB)
        return (pltpu.make_async_copy(wg_hbm.at[:, c], wgb.at[u % 2], gsem.at[u % 2]),
                pltpu.make_async_copy(wu_hbm.at[:, c], wub.at[u % 2], usem.at[u % 2]))

    def d_copy(d):
        k = d % 3
        half = (1 - core) if d < 3 else core
        c = pl.ds(mo(half * HALF + OFF[k], 128), WID[k])
        return pltpu.make_async_copy(
            wd_hbm.at[:, c], wdb.at[d % 2, :, pl.ds(0, WID[k])], dsem.at[d % 2])

    def y_copy(j, buf, half, which):
        return pltpu.make_async_copy(
            buf.at[j % YS],
            y_hbm.at[pl.ds(mo(j * M, M), M), pl.ds(mo(half * HALF, 128), HALF)],
            osem.at[which, j % YS])

    def d2d0(j, k):
        return rc(sb0.at[:, cols(k)], rb0.at[j % 2, :, cols(k)], ss0.at[k], rs0.at[j % 2, k], sib)

    def off1(g, p):
        (_, _), (bb, _), (bc, _) = g
        if p == 0:
            return mo((1 - bb) * 2 * PC, PC), 2 * PC
        if p == 1:
            return mo(bb * 2 * PC + (1 - bc) * PC, PC), PC
        return mo(bb * 2 * PC + bc * PC, PC), PC

    def c1(j, k, g, p):
        o, r = off1(g, p)
        return rc(s1.at[pl.ds(o, r), cols(k)], r1.at[j % 2, pl.ds(o, r), cols(k)],
                  ss1.at[k, p], rs1.at[j % 2, k, p], g[0][1])

    def off2(g, p):
        bc = g[2][0]
        return mo((1 - bc) * PC if p == 0 else bc * PC, PC)

    def c2(j, k, g, p):
        o = off2(g, p)
        return rc(s2.at[pl.ds(o, PC), cols(k)], r2.at[j % 2, pl.ds(o, PC), cols(k)],
                  ss2.at[k, p], rs2.at[j % 2, k, p], g[1][1])

    def c3(j, k, g):
        return rc(s3.at[:, cols(k)], r3.at[j % 2, :, cols(k)], ss3.at[k], rs3.at[j % 2, k], g[2][1])

    AG = (((0, 0, 0), 2), ((0, 0, 0), 1), ((0, 0, 0), 0),
          ((0, 0, 1), 1), ((0, 0, 1), 0), ((0, 1, 0), 0), ((0, 1, 1), 0))

    def off_g(g, f):
        v = 0
        for t, wgt in enumerate((4, 2, 1)):
            b = g[t][0]
            v = v + (1 - b if f[t] else b) * (wgt * PC)
        return mo(v, PC)

    def cg(j, k, g, q):
        f, t = AG[q]
        o = off_g(g, f)
        ref = yo.at[j % YS, pl.ds(o, PC), cols(k)]
        return rc(ref, ref, ssg.at[j % YS, k, q], rsg.at[j % YS, k, q], g[t][1])

    def cg_in(j, k, g, q):
        f, t = AG[q]
        f = tuple(1 - v if u == t else v for u, v in enumerate(f))
        o = off_g(g, f)
        ref = yo.at[j % YS, pl.ds(o, PC), cols(k)]
        return rc(ref, ref, ssg.at[j % YS, k, q], rsg.at[j % YS, k, q], g[t][1])

    def cd(j, k, g, p, mine=True):
        ba = g[0][0]
        o = mo((ba if p == 0 else 1 - ba) * 4 * PC, 4 * PC)
        return rc(yo.at[j % YS, pl.ds(o, 4 * PC), cols(k)], yb.at[j % YS, pl.ds(o, 4 * PC), cols(k)],
                  ssd.at[j % YS, k, p], rsd.at[j % YS, k, p], sib)

    def cd_in(j, k, p):
        return rc(yo.at[j % YS, pl.ds(0, 4 * PC), cols(k)], yb.at[j % YS, pl.ds(0, 4 * PC), cols(k)],
                  ssd.at[j % YS, k, p], rsd.at[j % YS, k, p], sib)

    def stage1(i, k):
        g = geo(i, k)
        ba = g[0][0]
        o = mo((1 - ba) * 4 * PC, 4 * PC)
        s1[:, cols(k)] = own[pl.ds(o, 4 * PC), cols(k)].astype(BF16)
        for p in range(3):
            c1(i, k, g, p).start()

    def own_rows(g, o, r):
        return pl.ds(mo(g[0][0] * 4 * PC + o, PC), r)

    def stage2(j):
        for k in range(3):
            g = geo(j, k)
            o, r = off1(g, 0)
            c1(j, k, g, 0).wait_recv()
            s2[:, cols(k)] = (own[own_rows(g, o, r), cols(k)]
                              + r1[j % 2, pl.ds(o, r), cols(k)].astype(F32)).astype(BF16)
            for p in range(2):
                c2(j, k, g, p).start()
        for k in range(3):
            d2d0(j, k).wait_send()

    def stage3(j):
        for k in range(3):
            g = geo(j, k)
            o, r = off1(g, 1)
            c1(j, k, g, 1).wait_recv()
            c2(j, k, g, 0).wait_recv()
            s3[:, cols(k)] = (own[own_rows(g, o, r), cols(k)]
                              + r1[j % 2, pl.ds(o, r), cols(k)].astype(F32)
                              + r2[j % 2, pl.ds(off2(g, 0), PC), cols(k)].astype(F32)).astype(BF16)
            c3(j, k, g).start()

    def stage4(j):
        for k in range(3):
            g = geo(j, k)
            o, r = off1(g, 2)
            c1(j, k, g, 2).wait_recv()
            c2(j, k, g, 1).wait_recv()
            c3(j, k, g).wait_recv()
            yo[j % YS, pl.ds(off_g(g, (0, 0, 0)), PC), cols(k)] = (
                own[own_rows(g, o, r), cols(k)]
                + r1[j % 2, pl.ds(o, r), cols(k)].astype(F32)
                + r2[j % 2, pl.ds(off2(g, 1), PC), cols(k)].astype(F32)
                + r3[j % 2, :, cols(k)].astype(F32)).astype(BF16)
            for q in range(3):
                cg(j, k, g, q).start()
        for k in range(3):
            g = geo(j, k)
            for p in range(3):
                c1(j, k, g, p).wait_send()
            for p in range(2):
                c2(j, k, g, p).wait_send()
            c3(j, k, g).wait_send()

    def stage5(j):
        for k in range(3):
            g = geo(j, k)
            cg_in(j, k, g, 0).wait_recv()
            cg(j, k, g, 3).start()
            cg(j, k, g, 4).start()
            cg_in(j, k, g, 1).wait_recv()
            cg(j, k, g, 5).start()

    def stage6(j):
        for k in range(3):
            g = geo(j, k)
            cg_in(j, k, g, 3).wait_recv()
            cg(j, k, g, 6).start()
            cd(j, k, g, 0).start()

    def stage7(j):
        for k in range(3):
            g = geo(j, k)
            for q in (2, 4, 5, 6):
                cg_in(j, k, g, q).wait_recv()
            cd(j, k, g, 1).start()
        y_copy(j, yo, core, 0).start()

    def stage8(j):
        for k in range(3):
            for p in range(2):
                cd_in(j, k, p).wait_recv()
        y_copy(j, yb, 1 - core, 1).start()

    def stage9(j):
        for k in range(3):
            g = geo(j, k)
            for q in range(7):
                cg(j, k, g, q).wait_send()
            for p in range(2):
                cd(j, k, g, p).wait_send()
        y_copy(j, yo, core, 0).wait()
        y_copy(j, yb, 1 - core, 1).wait()

    def at(i, lag, stage):
        j = i - lag

        @pl.when((j >= 0) & (j < n))
        def _():
            stage(j)

    x_copy(0).start()
    for u in range(2):
        for c in g_copies(u):
            c.start()
    barrier = pltpu.get_barrier_semaphore()
    for dev in [sib] + prts:
        pl.semaphore_signal(barrier, inc=1, device_id={"tp": dev}, device_id_type=MESH)
    pl.semaphore_wait(barrier, 4)

    def slot(i, carry):
        at(i, 3, stage9)

        @pl.when(i < n)
        def _():
            x_copy(i).wait()

        def gate_up(b, carry):
            @pl.when(i < n)
            def _():
                u = NG * i + b
                for c in g_copies(u):
                    c.wait()
                gate = jnp.dot(xb[i % 2], wgb[u % 2], preferred_element_type=F32)
                up = jnp.dot(xb[i % 2], wub[u % 2], preferred_element_type=F32)
                hid[:, pl.ds(mo(b * GB, GB), GB)] = (jax.nn.silu(gate) * up).astype(BF16)

                @pl.when(u + 2 < NG * n)
                def _():
                    for c in g_copies(u + 2):
                        c.start()

                @pl.when((u == 1))
                def _():
                    d_copy(0).start()
                    d_copy(1).start()

                @pl.when((b == 3) & (i + 1 < n))
                def _():
                    x_copy(i + 1).start()

            for pos, lag, stage in ((0, 2, stage5), (1, 1, stage2), (2, 2, stage6),
                                    (3, 1, stage3), (4, 2, stage7)):
                @pl.when(b == pos)
                def _():
                    at(i, lag, stage)
            return carry

        lax.fori_loop(0, NG, gate_up, 0)

        def down(d):
            d_copy(d).wait()
            out = jnp.dot(hid[...], wdb[d % 2, :, :WID[d % 3]], preferred_element_type=F32)
            return out

        def next_down(d):
            if d + 2 < 6:
                d_copy(d + 2).start()
            else:
                @pl.when(i + 1 < n)
                def _():
                    d_copy(d - 4).start()

        for d in range(3):
            @pl.when(i < n)
            def _():
                sb0[:, cols(d)] = down(d).astype(BF16)
                d2d0(i, d).start()
                next_down(d)
        at(i, 1, stage4)
        at(i, 2, stage8)
        for d in range(3, 6):
            @pl.when(i < n)
            def _():
                k = d - 3
                d2d0(i, k).wait_recv()
                own[:, cols(k)] = down(d) + rb0[i % 2, :, cols(k)].astype(F32)
                stage1(i, k)
                next_down(d)
        return carry

    lax.fori_loop(0, n + 3, slot, 0)


def solution(mesh):
    def step(x, w_gate, w_up, w_down):
        n = x.shape[0] // M
        dma = pltpu.SemaphoreType.DMA
        return pl.pallas_call(
            functools.partial(kernel, n),
            out_shape=jax.ShapeDtypeStruct(x.shape, BF16),
            in_specs=[pl.BlockSpec(memory_space=pl.ANY)] * 4,
            out_specs=pl.BlockSpec(memory_space=pl.ANY),
            scratch_shapes=[
                pltpu.VMEM((2, M, D), BF16),
                pltpu.VMEM((2, D, GB), BF16),
                pltpu.VMEM((2, D, GB), BF16),
                pltpu.VMEM((2, FF, max(WID)), BF16),
                pltpu.VMEM((M, FF), BF16),
                pltpu.VMEM((M, HALF), BF16),
                pltpu.VMEM((2, M, HALF), BF16),
                pltpu.VMEM((M, HALF), F32),
                pltpu.VMEM((M // 2, HALF), BF16),
                pltpu.VMEM((2, M // 2, HALF), BF16),
                pltpu.VMEM((M // 4, HALF), BF16),
                pltpu.VMEM((2, M // 4, HALF), BF16),
                pltpu.VMEM((M // 8, HALF), BF16),
                pltpu.VMEM((2, M // 8, HALF), BF16),
                pltpu.VMEM((YS, M, HALF), BF16),
                pltpu.VMEM((YS, M, HALF), BF16),
                dma((2,)), dma((2,)), dma((2,)), dma((2,)), dma((2, YS)),
                dma((3,)), dma((2, 3)),
                dma((3, 3)), dma((2, 3, 3)),
                dma((3, 2)), dma((2, 3, 2)),
                dma((3,)), dma((2, 3)),
                dma((YS, 3, 7)), dma((YS, 3, 7)),
                dma((YS, 3, 2)), dma((YS, 3, 2)),
            ],
            compiler_params=pltpu.CompilerParams(
                collective_id=0, has_side_effects=True, vmem_limit_bytes=66_000_000),
            name="mlp_ring",
        )(x, w_gate, w_up, w_down)

    return jax.shard_map(
        step,
        mesh=mesh,
        in_specs=(P("dp", None), P(None, "tp"), P(None, "tp"), P("tp", None)),
        out_specs=P("dp", None),
        check_vma=False,
    )
```

time: 460 us -> 285 us (0.62)
  waiting for transfers between devices: 284 us -> 0 us
  Pallas kernels: 0 us -> 264 us
  matrix products: 142 us -> 0 us
  between operations: 13.4 us -> 0.01 us
    psum x1 -> x0, waiting for transfers between devices: 284 us -> none  [step(): return lax.psum(term, 'tp')]
    pallas_call x0 -> x1, Pallas kernels: none -> 264 us  [step(): pl.pallas_call(functools.partial(kernel, n), out_shape=jax.ShapeDtypeStru...]
    dot_general x3 -> x0, matrix products: 142 us -> none  [the longest x1 48.1 us: step(): up = jnp.dot(x, w_up, preferred_element_type=jnp.float32)]
  transfers between devices with their start and end apart: 1 -> 0, of which waited for: 1 -> 0; matrix products, arithmetic and copies ran while one was open for 0% -> 0% of each run, Pallas kernels for 0% -> 0%
where the time goes in v1:
time: 285 us; the launch traced here: 284 us
  Pallas kernels  264 us (93%)
  local copies, waits for them, and re-layouts  20.2 us (7%)
    pallas_call x1, Pallas kernels, step(): pl.pallas_call(functools.partial(kernel, n), out_shape=jax.ShapeDtypeStru...  264 us
    unnamed x1, local copies, waits for them, and re-layouts  20.2 us

profile of v1, /device:TPU:0, one launch (start us, length us, event | category | flops | bytes accessed | tf_op | source)
XLA Modules:
  0.0 284.0 jit_solution(7906463717189875078)
XLA Ops:
  0.0 263.8 %mlp_ring.1 = bf16[2048,7168]{1,0:T(8,128)(2,1)} custom-call(bf16[2048,7168]{1,0:T(8,128)(2,1)} %x_hbm.1, bf16[7168,1280]{1,0:T(8,128)(2,1)} %wg_hbm.1, bf16[7168,1280]{1,0:T(8,128)(2,1)} %wu_hbm.1, bf16[1280,7168]{1,0:T(8,128)(2,1)} %wd_hbm.1), custom_call_target="tpu_custom_call" | custom-call | tf_op jit(solution)/shard_map/mlp_ring/pallas_call | solution.py:330
  263.8 20.2 %copy.6 = bf16[2048,7168]{1,0:T(8,128)(2,1)} copy(bf16[2048,7168]{1,0:T(8,128)(2,1)} %mlp_ring.1) | data formatting | bytes 58720256

commit v2 on v1

--- a/solution.py
+++ b/solution.py
@@ -56,7 +56,7 @@
 
     def x_copy(i):
         return pltpu.make_async_copy(
-            x_hbm.at[pl.ds(mo(i * M, M), M), :], xb.at[i % 2], xsem.at[i % 2])
+            x_hbm.at[pl.ds(mo(i * M, M), M), :], xb, xsem.at[0])
 
     def g_copies(u):
         c = pl.ds(mo((u % NG) * GB, GB), GB)
@@ -67,8 +67,7 @@
         k = d % 3
         half = (1 - core) if d < 3 else core
         c = pl.ds(mo(half * HALF + OFF[k], 128), WID[k])
-        return pltpu.make_async_copy(
-            wd_hbm.at[:, c], wdb.at[d % 2, :, pl.ds(0, WID[k])], dsem.at[d % 2])
+        return pltpu.make_async_copy(wd_hbm.at[:, c], wdb.at[d // 3, :, cols(k)], dsem.at[d])
 
     def y_copy(j, buf, half, which):
         return pltpu.make_async_copy(
@@ -250,8 +249,6 @@
     pl.semaphore_wait(barrier, 4)
 
     def slot(i, carry):
-        at(i, 3, stage9)
-
         @pl.when(i < n)
         def _():
             x_copy(i).wait()
@@ -262,8 +259,8 @@
                 u = NG * i + b
                 for c in g_copies(u):
                     c.wait()
-                gate = jnp.dot(xb[i % 2], wgb[u % 2], preferred_element_type=F32)
-                up = jnp.dot(xb[i % 2], wub[u % 2], preferred_element_type=F32)
+                gate = jnp.dot(xb[...], wgb[u % 2], preferred_element_type=F32)
+                up = jnp.dot(xb[...], wub[u % 2], preferred_element_type=F32)
                 hid[:, pl.ds(mo(b * GB, GB), GB)] = (jax.nn.silu(gate) * up).astype(BF16)
 
                 @pl.when(u + 2 < NG * n)
@@ -271,17 +268,18 @@
                     for c in g_copies(u + 2):
                         c.start()
 
-                @pl.when((u == 1))
-                def _():
-                    d_copy(0).start()
-                    d_copy(1).start()
-
-                @pl.when((b == 3) & (i + 1 < n))
+                for p, ds in ((1, (0,)), (2, (1,)), (3, (2,)), (4, (3, 4, 5))):
+                    @pl.when(u == p)
+                    def _():
+                        for d in ds:
+                            d_copy(d).start()
+
+                @pl.when((b == NG - 1) & (i + 1 < n))
                 def _():
                     x_copy(i + 1).start()
 
-            for pos, lag, stage in ((0, 2, stage5), (1, 1, stage2), (2, 2, stage6),
-                                    (3, 1, stage3), (4, 2, stage7)):
+            for pos, lag, stage in ((1, 1, stage2), (2, 2, stage5), (2, 3, stage8),
+                                    (3, 1, stage3), (4, 2, stage6), (4, 3, stage9)):
                 @pl.when(b == pos)
                 def _():
                     at(i, lag, stage)
@@ -290,34 +288,25 @@
         lax.fori_loop(0, NG, gate_up, 0)
 
         def down(d):
-            d_copy(d).wait()
-            out = jnp.dot(hid[...], wdb[d % 2, :, :WID[d % 3]], preferred_element_type=F32)
-            return out
-
-        def next_down(d):
-            if d + 2 < 6:
-                d_copy(d + 2).start()
-            else:
-                @pl.when(i + 1 < n)
-                def _():
-                    d_copy(d - 4).start()
+            @pl.when(i == 0)
+            def _():
+                d_copy(d).wait()
+            return jnp.dot(hid[...], wdb[d // 3, :, cols(d % 3)], preferred_element_type=F32)
 
         for d in range(3):
             @pl.when(i < n)
             def _():
                 sb0[:, cols(d)] = down(d).astype(BF16)
                 d2d0(i, d).start()
-                next_down(d)
-        at(i, 1, stage4)
-        at(i, 2, stage8)
-        for d in range(3, 6):
+            if d == 0:
+                at(i, 1, stage4)
+        for k in range(3):
             @pl.when(i < n)
             def _():
-                k = d - 3
                 d2d0(i, k).wait_recv()
-                own[:, cols(k)] = down(d) + rb0[i % 2, :, cols(k)].astype(F32)
+                own[:, cols(k)] = down(3 + k) + rb0[i % 2, :, cols(k)].astype(F32)
                 stage1(i, k)
-                next_down(d)
+        at(i, 2, stage7)
         return carry
 
     lax.fori_loop(0, n + 3, slot, 0)
@@ -333,10 +322,10 @@
             in_specs=[pl.BlockSpec(memory_space=pl.ANY)] * 4,
             out_specs=pl.BlockSpec(memory_space=pl.ANY),
             scratch_shapes=[
-                pltpu.VMEM((2, M, D), BF16),
+                pltpu.VMEM((M, D), BF16),
                 pltpu.VMEM((2, D, GB), BF16),
                 pltpu.VMEM((2, D, GB), BF16),
-                pltpu.VMEM((2, FF, max(WID)), BF16),
+                pltpu.VMEM((2, FF, HALF), BF16),
                 pltpu.VMEM((M, FF), BF16),
                 pltpu.VMEM((M, HALF), BF16),
                 pltpu.VMEM((2, M, HALF), BF16),
@@ -349,7 +338,7 @@
                 pltpu.VMEM((2, M // 8, HALF), BF16),
                 pltpu.VMEM((YS, M, HALF), BF16),
                 pltpu.VMEM((YS, M, HALF), BF16),
-                dma((2,)), dma((2,)), dma((2,)), dma((2,)), dma((2, YS)),
+                dma((1,)), dma((2,)), dma((2,)), dma((6,)), dma((2, YS)),
                 dma((3,)), dma((2, 3)),
                 dma((3, 3)), dma((2, 3, 3)),
                 dma((3, 2)), dma((2, 3, 2)),
@@ -358,7 +347,7 @@
                 dma((YS, 3, 2)), dma((YS, 3, 2)),
             ],
             compiler_params=pltpu.CompilerParams(
-                collective_id=0, has_side_effects=True, vmem_limit_bytes=66_000_000),
+                collective_id=0, has_side_effects=True, vmem_limit_bytes=67_043_328),
             name="mlp_ring",
         )(x, w_gate, w_up, w_down)
 

time: 285 us -> 245 us (0.86)
  Pallas kernels: 264 us -> 225 us
    pallas_call x1, Pallas kernels: 264 us -> 225 us  [step(): pl.pallas_call(functools.partial(kernel, n), out_shape=jax.ShapeDtypeStru...]
where the time goes in v2:
time: 245 us
  Pallas kernels  225 us (92%)
  local copies, waits for them, and re-layouts  20.2 us (8%)
    pallas_call x1, Pallas kernels, step(): pl.pallas_call(functools.partial(kernel, n), out_shape=jax.ShapeDtypeStru...  225 us
    unnamed x1, local copies, waits for them, and re-layouts  20.2 us

profile of v2, /device:TPU:0, one launch (start us, length us, event | category | flops | bytes accessed | tf_op | source)
XLA Modules:
  0.0 244.7 jit_solution(14128643327939135480)
XLA Ops:
  0.0 224.5 %mlp_ring.1 = bf16[2048,7168]{1,0:T(8,128)(2,1)} custom-call(bf16[2048,7168]{1,0:T(8,128)(2,1)} %x_hbm.1, bf16[7168,1280]{1,0:T(8,128)(2,1)} %wg_hbm.1, bf16[7168,1280]{1,0:T(8,128)(2,1)} %wu_hbm.1, bf16[1280,7168]{1,0:T(8,128)(2,1)} %wd_hbm.1), custom_call_target="tpu_custom_call" | custom-call | tf_op jit(solution)/shard_map/mlp_ring/pallas_call | solution.py:319
  224.6 20.2 %copy.6 = bf16[2048,7168]{1,0:T(8,128)(2,1)} copy(bf16[2048,7168]{1,0:T(8,128)(2,1)} %mlp_ring.1) | data formatting | bytes 58720256

commit v3 on v2

--- a/solution.py
+++ b/solution.py
@@ -15,6 +15,8 @@
 WID = (1280, 1152, 1152)
 GB = 256
 NG = FF // GB
+DH = D // 2
+GS = 3
 PC = M // 8
 YS = 3
 MESH = pl.DeviceIdType.MESH
@@ -22,8 +24,8 @@
 BF16 = jnp.bfloat16
 
 
-def kernel(n, x_hbm, wg_hbm, wu_hbm, wd_hbm, y_hbm,
-           xb, wgb, wub, wdb, hid, sb0, rb0, own, s1, r1, s2, r2, s3, r3, yo, yb,
+def kernel(n, x_hbm, wg_hbm, wu_hbm, wd_hbm, t_hbm, wdb, yo, yb,
+           xb, wgb, wub, hid, sb0, rb0, own, s1, r1, s2, r2, s3, r3,
            xsem, gsem, usem, dsem, osem,
            ss0, rs0, ss1, rs1, ss2, rs2, ss3, rs3, ssg, rsg, ssd, rsd):
     me = lax.axis_index("tp")
@@ -58,10 +60,11 @@
         return pltpu.make_async_copy(
             x_hbm.at[pl.ds(mo(i * M, M), M), :], xb, xsem.at[0])
 
-    def g_copies(u):
-        c = pl.ds(mo((u % NG) * GB, GB), GB)
-        return (pltpu.make_async_copy(wg_hbm.at[:, c], wgb.at[u % 2], gsem.at[u % 2]),
-                pltpu.make_async_copy(wu_hbm.at[:, c], wub.at[u % 2], usem.at[u % 2]))
+    def g_copies(v):
+        c = pl.ds(mo((v // 2) % NG * GB, GB), GB)
+        r = pl.ds(mo(v % 2 * DH, DH), DH)
+        return (pltpu.make_async_copy(wg_hbm.at[r, c], wgb.at[v % GS], gsem.at[v % GS]),
+                pltpu.make_async_copy(wu_hbm.at[r, c], wub.at[v % GS], usem.at[v % GS]))
 
     def d_copy(d):
         k = d % 3
@@ -71,9 +74,11 @@
 
     def y_copy(j, buf, half, which):
         return pltpu.make_async_copy(
-            buf.at[j % YS],
-            y_hbm.at[pl.ds(mo(j * M, M), M), pl.ds(mo(half * HALF, 128), HALF)],
-            osem.at[which, j % YS])
+            buf.at[j % YS], t_hbm.at[half, pl.ds(mo(j * M, M), M), :], osem.at[which, j % YS])
+
+    def t_copy(h):
+        r = (n - YS) * M
+        return pltpu.make_async_copy(t_hbm.at[h], wdb.at[h, pl.ds(0, r), :], dsem.at[h])
 
     def d2d0(j, k):
         return rc(sb0.at[:, cols(k)], rb0.at[j % 2, :, cols(k)], ss0.at[k], rs0.at[j % 2, k], sib)
@@ -214,13 +219,19 @@
             for q in (2, 4, 5, 6):
                 cg_in(j, k, g, q).wait_recv()
             cd(j, k, g, 1).start()
-        y_copy(j, yo, core, 0).start()
+
+        @pl.when(j < n - YS)
+        def _():
+            y_copy(j, yo, core, 0).start()
 
     def stage8(j):
         for k in range(3):
             for p in range(2):
                 cd_in(j, k, p).wait_recv()
-        y_copy(j, yb, 1 - core, 1).start()
+
+        @pl.when(j < n - YS)
+        def _():
+            y_copy(j, yb, 1 - core, 1).start()
 
     def stage9(j):
         for k in range(3):
@@ -229,8 +240,11 @@
                 cg(j, k, g, q).wait_send()
             for p in range(2):
                 cd(j, k, g, p).wait_send()
-        y_copy(j, yo, core, 0).wait()
-        y_copy(j, yb, 1 - core, 1).wait()
+
+        @pl.when(j < n - YS)
+        def _():
+            y_copy(j, yo, core, 0).wait()
+            y_copy(j, yb, 1 - core, 1).wait()
 
     def at(i, lag, stage):
         j = i - lag
@@ -240,8 +254,8 @@
             stage(j)
 
     x_copy(0).start()
-    for u in range(2):
-        for c in g_copies(u):
+    for v in range(GS):
+        for c in g_copies(v):
             c.start()
     barrier = pltpu.get_barrier_semaphore()
     for dev in [sib] + prts:
@@ -253,33 +267,42 @@
         def _():
             x_copy(i).wait()
 
+        @pl.when(i == n)
+        def _():
+            for h in range(2):
+                t_copy(h).start()
+
         def gate_up(b, carry):
             @pl.when(i < n)
             def _():
                 u = NG * i + b
-                for c in g_copies(u):
-                    c.wait()
-                gate = jnp.dot(xb[...], wgb[u % 2], preferred_element_type=F32)
-                up = jnp.dot(xb[...], wub[u % 2], preferred_element_type=F32)
+                gate = up = 0.0
+                for h in range(2):
+                    v = 2 * u + h
+                    for c in g_copies(v):
+                        c.wait()
+                    xh = xb[:, h * DH:(h + 1) * DH]
+                    gate += jnp.dot(xh, wgb[v % GS], preferred_element_type=F32)
+                    up += jnp.dot(xh, wub[v % GS], preferred_element_type=F32)
+
+                    @pl.when((v + GS < 2 * NG * n) & ((i > 0) | (v + GS < 2 * NG)))
+                    def _():
+                        for c in g_copies(v + GS):
+                            c.start()
                 hid[:, pl.ds(mo(b * GB, GB), GB)] = (jax.nn.silu(gate) * up).astype(BF16)
 
-                @pl.when(u + 2 < NG * n)
-                def _():
-                    for c in g_copies(u + 2):
-                        c.start()
-
-                for p, ds in ((1, (0,)), (2, (1,)), (3, (2,)), (4, (3, 4, 5))):
+                for p, ds in ((2, (0, 1)), (3, (2, 3)), (4, (4, 5))):
                     @pl.when(u == p)
                     def _():
                         for d in ds:
                             d_copy(d).start()
 
-                @pl.when((b == NG - 1) & (i + 1 < n))
+                @pl.when((b == NG - 1) & (i > 0) & (i + 1 < n))
                 def _():
                     x_copy(i + 1).start()
 
-            for pos, lag, stage in ((1, 1, stage2), (2, 2, stage5), (2, 3, stage8),
-                                    (3, 1, stage3), (4, 2, stage6), (4, 3, stage9)):
+            for pos, lag, stage in ((1, 1, stage2), (1, 3, stage6), (3, 1, stage3),
+                                    (3, 2, stage5), (3, 3, stage7), (4, 3, stage8)):
                 @pl.when(b == pos)
                 def _():
                     at(i, lag, stage)
@@ -299,33 +322,63 @@
                 sb0[:, cols(d)] = down(d).astype(BF16)
                 d2d0(i, d).start()
             if d == 0:
+                at(i, 3, stage9)
                 at(i, 1, stage4)
+
+        @pl.when(i == 0)
+        def _():
+            x_copy(1).start()
+            for v in range(2 * NG, 2 * NG + GS):
+                for c in g_copies(v):
+                    c.start()
+
         for k in range(3):
             @pl.when(i < n)
             def _():
                 d2d0(i, k).wait_recv()
                 own[:, cols(k)] = down(3 + k) + rb0[i % 2, :, cols(k)].astype(F32)
                 stage1(i, k)
-        at(i, 2, stage7)
         return carry
 
     lax.fori_loop(0, n + 3, slot, 0)
+    for h in range(2):
+        t_copy(h).wait()
+
+
+def finish(n, wdb, yo, yb, y_hbm, sem):
+    core = lax.axis_index("tp") % 2
+    outs = []
+    for j in range(n):
+        for h in range(2):
+            rows = pl.ds(j * M, M)
+            if j < n - YS:
+                src, half = wdb.at[h, rows, :], h
+            else:
+                src, half = (yo, yb)[h].at[j % YS], (core, 1 - core)[h]
+            dst = y_hbm.at[rows, pl.ds(pl.multiple_of(half * HALF, 128), HALF)]
+            outs.append(pltpu.make_async_copy(src, dst, sem.at[j, h]))
+            outs[-1].start()
+    for c in outs:
+        c.wait()
 
 
 def solution(mesh):
     def step(x, w_gate, w_up, w_down):
         n = x.shape[0] // M
+        assert n > YS and (n - YS) * M <= FF
         dma = pltpu.SemaphoreType.DMA
-        return pl.pallas_call(
+        vmem = pl.BlockSpec(memory_space=pltpu.VMEM)
+        part = pltpu.VMEM((YS, M, HALF), BF16)
+        outs = pl.pallas_call(
             functools.partial(kernel, n),
-            out_shape=jax.ShapeDtypeStruct(x.shape, BF16),
+            out_shape=(jax.ShapeDtypeStruct((2, (n - YS) * M, HALF), BF16),
+                       pltpu.VMEM((2, FF, HALF), BF16), part, part),
             in_specs=[pl.BlockSpec(memory_space=pl.ANY)] * 4,
-            out_specs=pl.BlockSpec(memory_space=pl.ANY),
+            out_specs=(pl.BlockSpec(memory_space=pl.ANY), vmem, vmem, vmem),
             scratch_shapes=[
                 pltpu.VMEM((M, D), BF16),
-                pltpu.VMEM((2, D, GB), BF16),
-                pltpu.VMEM((2, D, GB), BF16),
-                pltpu.VMEM((2, FF, HALF), BF16),
+                pltpu.VMEM((GS, DH, GB), BF16),
+                pltpu.VMEM((GS, DH, GB), BF16),
                 pltpu.VMEM((M, FF), BF16),
                 pltpu.VMEM((M, HALF), BF16),
                 pltpu.VMEM((2, M, HALF), BF16),
@@ -336,9 +389,7 @@
                 pltpu.VMEM((2, M // 4, HALF), BF16),
                 pltpu.VMEM((M // 8, HALF), BF16),
                 pltpu.VMEM((2, M // 8, HALF), BF16),
-                pltpu.VMEM((YS, M, HALF), BF16),
-                pltpu.VMEM((YS, M, HALF), BF16),
-                dma((1,)), dma((2,)), dma((2,)), dma((6,)), dma((2, YS)),
+                dma((1,)), dma((GS,)), dma((GS,)), dma((6,)), dma((2, YS)),
                 dma((3,)), dma((2, 3)),
                 dma((3, 3)), dma((2, 3, 3)),
                 dma((3, 2)), dma((2, 3, 2)),
@@ -347,9 +398,18 @@
                 dma((YS, 3, 2)), dma((YS, 3, 2)),
             ],
             compiler_params=pltpu.CompilerParams(
-                collective_id=0, has_side_effects=True, vmem_limit_bytes=67_043_328),
+                collective_id=0, has_side_effects=True, vmem_limit_bytes=37_500_000),
             name="mlp_ring",
         )(x, w_gate, w_up, w_down)
+        return pl.pallas_call(
+            functools.partial(finish, n),
+            out_shape=jax.ShapeDtypeStruct(x.shape, BF16),
+            in_specs=[vmem] * 3,
+            out_specs=pl.BlockSpec(memory_space=pl.ANY),
+            scratch_shapes=[dma((n, 2))],
+            compiler_params=pltpu.CompilerParams(vmem_limit_bytes=1_000_000),
+            name="finish",
+        )(*outs[1:])
 
     return jax.shard_map(
         step,

time: 245 us -> 233 us (0.951)
  local copies, waits for them, and re-layouts: 20.2 us -> 0 us
  Pallas kernels: 225 us -> 233 us
    unnamed x1 -> x0, local copies, waits for them, and re-layouts: 20.2 us -> none
    pallas_call x1 -> x2, Pallas kernels: 225 us -> 233 us  [the longest x1 223 us: step(): pl.pallas_call(functools.partial(kernel, n), out_shape=(jax.ShapeDtypeStr...]
where the time goes in v3:
time: 233 us
  Pallas kernels  233 us (100%)
    pallas_call x1, Pallas kernels, step(): pl.pallas_call(functools.partial(kernel, n), out_shape=(jax.ShapeDtypeStr...  223 us
    pallas_call x1, Pallas kernels, step(): pl.pallas_call(functools.partial(finish, n), out_shape=jax.ShapeDtypeStru...  9.8 us

profile of v3, /device:TPU:0, one launch (start us, length us, event | category | flops | bytes accessed | tf_op | source)
XLA Modules:
  0.0 232.8 jit_solution(9124073313236660240)
XLA Ops:
  0.0 223.0 %mlp_ring.1 = (bf16[2,1280,3584]{2,1,0:T(8,128)(2,1)}, bf16[2,1280,3584]{2,1,0:T(8,128)(2,1)S(1)}, bf16[3,256,3584]{2,1,0:T(8,128)(2,1)S(1)}, bf16[3,256,3584]{2,1,0:T(8,128)(2,1)S(1)}) custom-call(bf16[2048,7168]{1,0:T(8,128)(2,1)} %x_hbm.1, bf16[7168,1280]{1,0:T(8,128)(2,1)} %wg_hbm.1, bf16[7168,1280]{1,0:T(8,128)(2,1)} %wu_hbm.1, bf16[1280,7168]{1,0:T(8,128)(2,1)} %wd_hbm.1), custom_call_target="tpu_custom_call" | custom-call | tf_op jit(solution)/shard_map/mlp_ring/pallas_call | solution.py:372
  223.0 9.8 %finish.1 = bf16[2048,7168]{1,0:T(8,128)(2,1)} custom-call(bf16[2,1280,3584]{2,1,0:T(8,128)(2,1)S(1)} %get-tuple-element.8.wdb, bf16[3,256,3584]{2,1,0:T(8,128)(2,1)S(1)} %get-tuple-element.9.yo, bf16[3,256,3584]{2,1,0:T(8,128)(2,1)S(1)} %get-tuple-element.10.yb), custom_call_target="tpu_custom_call" | custom-call | tf_op jit(solution)/shard_map/finish/pallas_call | solution.py:404

commit v4 on v3

--- a/solution.py
+++ b/solution.py
@@ -152,88 +152,75 @@
     def own_rows(g, o, r):
         return pl.ds(mo(g[0][0] * 4 * PC + o, PC), r)
 
-    def stage2(j):
-        for k in range(3):
-            g = geo(j, k)
-            o, r = off1(g, 0)
-            c1(j, k, g, 0).wait_recv()
-            s2[:, cols(k)] = (own[own_rows(g, o, r), cols(k)]
-                              + r1[j % 2, pl.ds(o, r), cols(k)].astype(F32)).astype(BF16)
-            for p in range(2):
-                c2(j, k, g, p).start()
-        for k in range(3):
-            d2d0(j, k).wait_send()
-
-    def stage3(j):
-        for k in range(3):
-            g = geo(j, k)
-            o, r = off1(g, 1)
-            c1(j, k, g, 1).wait_recv()
-            c2(j, k, g, 0).wait_recv()
-            s3[:, cols(k)] = (own[own_rows(g, o, r), cols(k)]
-                              + r1[j % 2, pl.ds(o, r), cols(k)].astype(F32)
-                              + r2[j % 2, pl.ds(off2(g, 0), PC), cols(k)].astype(F32)).astype(BF16)
-            c3(j, k, g).start()
-
-    def stage4(j):
-        for k in range(3):
-            g = geo(j, k)
-            o, r = off1(g, 2)
-            c1(j, k, g, 2).wait_recv()
-            c2(j, k, g, 1).wait_recv()
-            c3(j, k, g).wait_recv()
-            yo[j % YS, pl.ds(off_g(g, (0, 0, 0)), PC), cols(k)] = (
-                own[own_rows(g, o, r), cols(k)]
-                + r1[j % 2, pl.ds(o, r), cols(k)].astype(F32)
-                + r2[j % 2, pl.ds(off2(g, 1), PC), cols(k)].astype(F32)
-                + r3[j % 2, :, cols(k)].astype(F32)).astype(BF16)
-            for q in range(3):
-                cg(j, k, g, q).start()
-        for k in range(3):
-            g = geo(j, k)
-            for p in range(3):
-                c1(j, k, g, p).wait_send()
-            for p in range(2):
-                c2(j, k, g, p).wait_send()
-            c3(j, k, g).wait_send()
-
-    def stage5(j):
-        for k in range(3):
-            g = geo(j, k)
-            cg_in(j, k, g, 0).wait_recv()
-            cg(j, k, g, 3).start()
-            cg(j, k, g, 4).start()
-            cg_in(j, k, g, 1).wait_recv()
-            cg(j, k, g, 5).start()
-
-    def stage6(j):
-        for k in range(3):
-            g = geo(j, k)
-            cg_in(j, k, g, 3).wait_recv()
-            cg(j, k, g, 6).start()
-            cd(j, k, g, 0).start()
-
-    def stage7(j):
-        for k in range(3):
-            g = geo(j, k)
-            for q in (2, 4, 5, 6):
-                cg_in(j, k, g, q).wait_recv()
-            cd(j, k, g, 1).start()
-
+    def stage2(j, k):
+        g = geo(j, k)
+        o, r = off1(g, 0)
+        c1(j, k, g, 0).wait_recv()
+        s2[:, cols(k)] = (own[own_rows(g, o, r), cols(k)]
+                          + r1[j % 2, pl.ds(o, r), cols(k)].astype(F32)).astype(BF16)
+        for p in range(2):
+            c2(j, k, g, p).start()
+        d2d0(j, k).wait_send()
+
+    def stage3(j, k):
+        g = geo(j, k)
+        o, r = off1(g, 1)
+        c1(j, k, g, 1).wait_recv()
+        c2(j, k, g, 0).wait_recv()
+        s3[:, cols(k)] = (own[own_rows(g, o, r), cols(k)]
+                          + r1[j % 2, pl.ds(o, r), cols(k)].astype(F32)
+                          + r2[j % 2, pl.ds(off2(g, 0), PC), cols(k)].astype(F32)).astype(BF16)
+        c3(j, k, g).start()
+
+    def stage4(j, k):
+        g = geo(j, k)
+        o, r = off1(g, 2)
+        c1(j, k, g, 2).wait_recv()
+        c2(j, k, g, 1).wait_recv()
+        c3(j, k, g).wait_recv()
+        yo[j % YS, pl.ds(off_g(g, (0, 0, 0)), PC), cols(k)] = (
+            own[own_rows(g, o, r), cols(k)]
+            + r1[j % 2, pl.ds(o, r), cols(k)].astype(F32)
+            + r2[j % 2, pl.ds(off2(g, 1), PC), cols(k)].astype(F32)
+            + r3[j % 2, :, cols(k)].astype(F32)).astype(BF16)
+        for q in range(3):
+            cg(j, k, g, q).start()
+        for p in range(3):
+            c1(j, k, g, p).wait_send()
+        for p in range(2):
+            c2(j, k, g, p).wait_send()
+        c3(j, k, g).wait_send()
+
+    def stage5(j, k):
+        g = geo(j, k)
+        cg_in(j, k, g, 0).wait_recv()
+        cg(j, k, g, 3).start()
+        cg(j, k, g, 4).start()
+        cg_in(j, k, g, 1).wait_recv()
+        cg(j, k, g, 5).start()
+
+    def stage6(j, k):
+        g = geo(j, k)
+        cg_in(j, k, g, 3).wait_recv()
+        cg(j, k, g, 6).start()
+        cd(j, k, g, 0).start()
+
+    def stage7(j, k):
+        g = geo(j, k)
+        for q in (2, 4, 5, 6):
+            cg_in(j, k, g, q).wait_recv()
+        cd(j, k, g, 1).start()
+
+    def stage8(j, k):
+        for p in range(2):
+            cd_in(j, k, p).wait_recv()
+
+    def store(j, which):
         @pl.when(j < n - YS)
         def _():
-            y_copy(j, yo, core, 0).start()
-
-    def stage8(j):
-        for k in range(3):
-            for p in range(2):
-                cd_in(j, k, p).wait_recv()
-
-        @pl.when(j < n - YS)
-        def _():
-            y_copy(j, yb, 1 - core, 1).start()
-
-    def stage9(j):
+            y_copy(j, (yo, yb)[which], (core, 1 - core)[which], which).start()
+
+    def stage9(j, _):
         for k in range(3):
             g = geo(j, k)
             for q in range(7):
@@ -246,12 +233,26 @@
             y_copy(j, yo, core, 0).wait()
             y_copy(j, yb, 1 - core, 1).wait()
 
-    def at(i, lag, stage):
-        j = i - lag
-
-        @pl.when((j >= 0) & (j < n))
-        def _():
-            stage(j)
+    plan = {
+        1: ((1, stage2, 1), (1, stage2, 0), (1, stage2, 2)),
+        2: ((2, stage5, 0), (3, stage7, 1), (2, stage5, 1)),
+        3: ((1, stage3, 2), (1, stage3, 0), (3, stage7, 0), (2, stage5, 2), (3, stage7, 2),
+            (3, store, 0), (3, stage8, 0)),
+        4: ((3, stage8, 1), (3, stage8, 2), (3, store, 1), (1, stage3, 1)),
+        5: ((3, stage9, 0), (1, stage4, 2), (2, stage6, 1)),
+        6: ((1, stage4, 0),),
+        7: ((1, stage4, 1),),
+        8: ((2, stage6, 0),),
+        9: ((2, stage6, 2),),
+    }
+
+    def at(i, pos):
+        for lag, stage, k in plan.get(pos, ()):
+            j = i - lag
+
+            @pl.when((j >= 0) & (j < n))
+            def _():
+                stage(j, k)
 
     x_copy(0).start()
     for v in range(GS):
@@ -291,7 +292,7 @@
                             c.start()
                 hid[:, pl.ds(mo(b * GB, GB), GB)] = (jax.nn.silu(gate) * up).astype(BF16)
 
-                for p, ds in ((2, (0, 1)), (3, (2, 3)), (4, (4, 5))):
+                for p, ds in ((2, (0,)), (3, (1, 2, 3)), (4, (4, 5))):
                     @pl.when(u == p)
                     def _():
                         for d in ds:
@@ -301,11 +302,10 @@
                 def _():
                     x_copy(i + 1).start()
 
-            for pos, lag, stage in ((1, 1, stage2), (1, 3, stage6), (3, 1, stage3),
-                                    (3, 2, stage5), (3, 3, stage7), (4, 3, stage8)):
+            for pos in range(NG):
                 @pl.when(b == pos)
                 def _():
-                    at(i, lag, stage)
+                    at(i, pos)
             return carry
 
         lax.fori_loop(0, NG, gate_up, 0)
@@ -321,16 +321,14 @@
             def _():
                 sb0[:, cols(d)] = down(d).astype(BF16)
                 d2d0(i, d).start()
-            if d == 0:
-                at(i, 3, stage9)
-                at(i, 1, stage4)
-
-        @pl.when(i == 0)
-        def _():
-            x_copy(1).start()
-            for v in range(2 * NG, 2 * NG + GS):
-                for c in g_copies(v):
-                    c.start()
+            at(i, NG + d)
+            if d == 1:
+                @pl.when(i == 0)
+                def _():
+                    x_copy(1).start()
+                    for v in range(2 * NG, 2 * NG + GS):
+                        for c in g_copies(v):
+                            c.start()
 
         for k in range(3):
             @pl.when(i < n)
@@ -338,6 +336,7 @@
                 d2d0(i, k).wait_recv()
                 own[:, cols(k)] = down(3 + k) + rb0[i % 2, :, cols(k)].astype(F32)
                 stage1(i, k)
+            at(i, NG + 3 + k)
         return carry
 
     lax.fori_loop(0, n + 3, slot, 0)

time: 233 us -> 230 us (0.987)
  Pallas kernels: 233 us -> 230 us
    pallas_call x1, Pallas kernels: 223 us -> 220 us  [step(): pl.pallas_call(functools.partial(kernel, n), out_shape=(jax.ShapeDtypeStr...]
where the time goes in v4:
time: 230 us
  Pallas kernels  230 us (100%)
    pallas_call x1, Pallas kernels, step(): pl.pallas_call(functools.partial(kernel, n), out_shape=(jax.ShapeDtypeStr...  220 us
    pallas_call x1, Pallas kernels, step(): pl.pallas_call(functools.partial(finish, n), out_shape=jax.ShapeDtypeStru...  9.8 us

profile of v4, /device:TPU:0, one launch (start us, length us, event | category | flops | bytes accessed | tf_op | source)
XLA Modules:
  0.0 230.0 jit_solution(8211684551223589965)
XLA Ops:
  0.0 220.2 %mlp_ring.1 = (bf16[2,1280,3584]{2,1,0:T(8,128)(2,1)}, bf16[2,1280,3584]{2,1,0:T(8,128)(2,1)S(1)}, bf16[3,256,3584]{2,1,0:T(8,128)(2,1)S(1)}, bf16[3,256,3584]{2,1,0:T(8,128)(2,1)S(1)}) custom-call(bf16[2048,7168]{1,0:T(8,128)(2,1)} %x_hbm.1, bf16[7168,1280]{1,0:T(8,128)(2,1)} %wg_hbm.1, bf16[7168,1280]{1,0:T(8,128)(2,1)} %wu_hbm.1, bf16[1280,7168]{1,0:T(8,128)(2,1)} %wd_hbm.1), custom_call_target="tpu_custom_call" | custom-call | tf_op jit(solution)/shard_map/mlp_ring/pallas_call | solution.py:371
  220.2 9.8 %finish.1 = bf16[2048,7168]{1,0:T(8,128)(2,1)} custom-call(bf16[2,1280,3584]{2,1,0:T(8,128)(2,1)S(1)} %get-tuple-element.8.wdb, bf16[3,256,3584]{2,1,0:T(8,128)(2,1)S(1)} %get-tuple-element.9.yo, bf16[3,256,3584]{2,1,0:T(8,128)(2,1)S(1)} %get-tuple-element.10.yb), custom_call_target="tpu_custom_call" | custom-call | tf_op jit(solution)/shard_map/finish/pallas_call | solution.py:403

commit v5 on v4

--- a/solution.py
+++ b/solution.py
@@ -234,16 +234,15 @@
             y_copy(j, yb, 1 - core, 1).wait()
 
     plan = {
-        1: ((1, stage2, 1), (1, stage2, 0), (1, stage2, 2)),
-        2: ((2, stage5, 0), (3, stage7, 1), (2, stage5, 1)),
-        3: ((1, stage3, 2), (1, stage3, 0), (3, stage7, 0), (2, stage5, 2), (3, stage7, 2),
-            (3, store, 0), (3, stage8, 0)),
-        4: ((3, stage8, 1), (3, stage8, 2), (3, store, 1), (1, stage3, 1)),
+        1: ((1, stage2, 0), (1, stage2, 1), (3, stage7, 1), (1, stage2, 2)),
+        2: ((2, stage5, 0), (2, stage5, 1), (3, stage7, 0)),
+        3: ((1, stage3, 2), (3, stage7, 2), (1, stage3, 0), (2, stage5, 2), (1, stage3, 1),
+            (3, store, 0)),
+        4: ((3, stage8, 2), (3, stage8, 1), (3, stage8, 0), (3, store, 1)),
         5: ((3, stage9, 0), (1, stage4, 2), (2, stage6, 1)),
         6: ((1, stage4, 0),),
-        7: ((1, stage4, 1),),
-        8: ((2, stage6, 0),),
-        9: ((2, stage6, 2),),
+        7: ((1, stage4, 1), (2, stage6, 0)),
+        8: ((2, stage6, 2),),
     }
 
     def at(i, pos):

time: 230 us -> 230 us (level)
  no operation moved by 1% of the time
where the time goes in v5:
time: 230 us
  Pallas kernels  230 us (100%)
    pallas_call x1, Pallas kernels, step(): pl.pallas_call(functools.partial(kernel, n), out_shape=(jax.ShapeDtypeStr...  220 us
    pallas_call x1, Pallas kernels, step(): pl.pallas_call(functools.partial(finish, n), out_shape=jax.ShapeDtypeStru...  9.8 us

profile of v5, /device:TPU:0, one launch (start us, length us, event | category | flops | bytes accessed | tf_op | source)
XLA Modules:
  0.0 229.8 jit_solution(9966061846579676566)
XLA Ops:
  0.0 220.0 %mlp_ring.1 = (bf16[2,1280,3584]{2,1,0:T(8,128)(2,1)}, bf16[2,1280,3584]{2,1,0:T(8,128)(2,1)S(1)}, bf16[3,256,3584]{2,1,0:T(8,128)(2,1)S(1)}, bf16[3,256,3584]{2,1,0:T(8,128)(2,1)S(1)}) custom-call(bf16[2048,7168]{1,0:T(8,128)(2,1)} %x_hbm.1, bf16[7168,1280]{1,0:T(8,128)(2,1)} %wg_hbm.1, bf16[7168,1280]{1,0:T(8,128)(2,1)} %wu_hbm.1, bf16[1280,7168]{1,0:T(8,128)(2,1)} %wd_hbm.1), custom_call_target="tpu_custom_call" | custom-call | tf_op jit(solution)/shard_map/mlp_ring/pallas_call | solution.py:370
  220.0 9.8 %finish.1 = bf16[2048,7168]{1,0:T(8,128)(2,1)} custom-call(bf16[2,1280,3584]{2,1,0:T(8,128)(2,1)S(1)} %get-tuple-element.8.wdb, bf16[3,256,3584]{2,1,0:T(8,128)(2,1)S(1)} %get-tuple-element.9.yo, bf16[3,256,3584]{2,1,0:T(8,128)(2,1)S(1)} %get-tuple-element.10.yb), custom_call_target="tpu_custom_call" | custom-call | tf_op jit(solution)/shard_map/finish/pallas_call | solution.py:402
